TPU v7x, 256 devices: a whole 4x4x8 slice. The times are simulated.
256 devices in a mesh: crop: 4 (over z_hi, core), row: 64 (over y, x, z_lo).
Axes of the slice: x: 4, y: 4, z: 8 (z_hi: 2, z_lo: 4; z = z_hi * 4 + z_lo), core: 2. Of those that a mesh axis runs over, the one named last changes fastest.
Arguments:
- pair: bfloat16 [4, 512, 512, 128], P('crop', 'row'), may hold values from -6 to 6
- cotangent: bfloat16 [4, 512, 512, 128], P('crop', 'row'), may hold values from -6 to 6
- lengths: int32 [4], P('crop'), may hold values from 256 to 512
- proj_weight: bfloat16 [128, 640], replicated, may hold values from -0.5 to 0.5
- out_weight: bfloat16 [128, 128], replicated, may hold values from -0.5 to 0.5
- up_weight: bfloat16 [128, 512], replicated, may hold values from -0.5 to 0.5
- down_weight: bfloat16 [512, 128], replicated, may hold values from -0.25 to 0.25
- norm_gain: float32 [3, 128], replicated, may hold values from 0.1 to 1.9
- norm_bias: float32 [3, 128], replicated, may hold values from -3 to 3
Outputs:
- grad_pair: bfloat16 [4, 512, 512, 128], P('crop', 'row')
- grad_proj: float32 [128, 640], replicated
- grad_out: float32 [128, 128], replicated
- grad_up: float32 [128, 512], replicated
- grad_down: float32 [512, 128], replicated
- grad_gain: float32 [3, 128], replicated
- grad_bias: float32 [3, 128], replicated
Inputs may be any that keep to these rules, and one draw needn't show every extreme that they name: lengths[s] residues of crop s are present; the rest are masked.
All inputs are finite; a program needn't handle non-finite values.
Results may differ from a plain program's by a relative error of at most 0.009.
Values may be sent and summed in bfloat16 or wider, within the bound.
A program may use at most 128 MiB of HBM per device.

v0:
```python
import jax
import jax.numpy as jnp
from jax import lax
from jax.sharding import PartitionSpec as P

EPSILON = 1e-05


def side_by_side(arrays, axis, split_dim, concat_dim, along):
    widths = [a.shape[along] for a in arrays]
    both = jnp.concatenate(arrays, axis=along)
    filled = lax.all_to_all(both, axis, split_axis=split_dim, concat_axis=concat_dim, tiled=True)
    return tuple(jnp.split(filled, [sum(widths[:k]) for k in range(1, len(widths))], axis=along))


def together(arrays, axis):
    vector, at, outs = (jnp.concatenate([a.reshape(-1) for a in arrays]), 0, [])
    total = lax.psum(vector, axis)
    for a in arrays:
        outs.append(total[at : at + a.size].reshape(a.shape))
        at += a.size
    return tuple(outs)


def for_sending(x):
    return jax.tree.map(lambda a: a.astype(jnp.bfloat16) if a.dtype == jnp.float32 else a, x)


def contract(pattern, left_side, right_side):
    return jnp.einsum(pattern, left_side, right_side, preferred_element_type=jnp.float32)


def norm_forward(values, gain_vec, bias_vec, norm_axis):
    center = values - jnp.mean(values, axis=norm_axis, keepdims=True)
    inv_std = lax.rsqrt(jnp.mean(center * center, axis=norm_axis, keepdims=True) + EPSILON)
    normed = center * inv_std
    return (normed, inv_std, normed * gain_vec + bias_vec)


def norm_backward(upstream, normed, inv_std, gain_vec, norm_axis, others):
    grad_gain = jnp.sum(upstream * normed, axis=others)
    grad_bias = jnp.sum(upstream, axis=others)
    scaled = upstream * gain_vec
    result = inv_std * (
        scaled
        - jnp.mean(scaled, axis=norm_axis, keepdims=True)
        - normed * jnp.mean(scaled * normed, axis=norm_axis, keepdims=True)
    )
    return (result, grad_gain, grad_bias)


def enter_rows(pair_rows, row_keep, col_keep, proj_weight, norm_gain, norm_bias):
    channels = pair_rows.shape[2]
    normed_in, inv_in, scaled_in = norm_forward(
        pair_rows.astype(jnp.float32), norm_gain[0], norm_bias[0], 2
    )
    input_bf = scaled_in.astype(jnp.bfloat16)
    factor_pre = contract("rld,de->erl", input_bf, proj_weight[:, : 4 * channels])
    gate_pre = contract("rld,de->rle", input_bf, proj_weight[:, 4 * channels :])
    keep_both = row_keep[:, None] * col_keep[None, :]
    left_bf = (
        jax.nn.sigmoid(factor_pre[:channels]) * factor_pre[channels : 2 * channels] * keep_both
    ).astype(jnp.bfloat16)
    right_bf = (
        jax.nn.sigmoid(factor_pre[2 * channels : 3 * channels])
        * factor_pre[3 * channels :]
        * keep_both
    ).astype(jnp.bfloat16)
    return (input_bf, normed_in, inv_in, factor_pre, gate_pre, keep_both, left_bf, right_bf)


def middle_rows(
    pair_rows,
    cot_rows,
    product_bf,
    gate_pre,
    out_weight,
    up_weight,
    down_weight,
    norm_gain,
    norm_bias,
):
    prod_normed, prod_inv, prod_scaled = norm_forward(
        product_bf.astype(jnp.float32), norm_gain[1][:, None, None], norm_bias[1][:, None, None], 0
    )
    prod_norm_bf = prod_scaled.astype(jnp.bfloat16)
    update = contract("crj,cd->rjd", prod_norm_bf, out_weight)
    gate_sig = jax.nn.sigmoid(gate_pre)
    first_bf = (pair_rows.astype(jnp.float32) + gate_sig * update).astype(jnp.bfloat16)
    tran_normed, tran_inv, tran_scaled = norm_forward(
        first_bf.astype(jnp.float32), norm_gain[2], norm_bias[2], 2
    )
    tran_bf = tran_scaled.astype(jnp.bfloat16)
    hidden_pre = contract("rld,dh->rlh", tran_bf, up_weight)
    hidden_sig = jax.nn.sigmoid(hidden_pre)
    hidden_bf = (hidden_pre * hidden_sig).astype(jnp.bfloat16)
    grad_down = contract("rlh,rld->hd", hidden_bf, cot_rows)
    hidden_grad_bf = (
        contract("rld,hd->rlh", cot_rows, down_weight)
        * hidden_sig
        * (1.0 + hidden_pre * (1.0 - hidden_sig))
    ).astype(jnp.bfloat16)
    grad_up = contract("rld,rlh->dh", tran_bf, hidden_grad_bf)
    tran_grad = contract("rlh,dh->rld", hidden_grad_bf, up_weight)
    first_grad, gain_tran, bias_tran = norm_backward(
        tran_grad, tran_normed, tran_inv, norm_gain[2], 2, (0, 1)
    )
    first_grad = first_grad + cot_rows.astype(jnp.float32)
    update_grad_bf = (first_grad * gate_sig).astype(jnp.bfloat16)
    gate_grad_bf = (first_grad * update * gate_sig * (1.0 - gate_sig)).astype(jnp.bfloat16)
    grad_out = contract("crj,rjd->cd", prod_norm_bf, update_grad_bf)
    norm_grad = contract("rjd,cd->crj", update_grad_bf, out_weight)
    prod_grad, gain_prod, bias_prod = norm_backward(
        norm_grad, prod_normed, prod_inv, norm_gain[1][:, None, None], 0, (1, 2)
    )
    return (
        prod_grad.astype(jnp.bfloat16),
        first_grad,
        gate_grad_bf,
        grad_out,
        grad_up,
        grad_down,
        gain_prod,
        bias_prod,
        gain_tran,
        bias_tran,
    )


def leave_rows(
    left_grad,
    right_grad,
    factor_pre,
    keep_both,
    gate_grad_bf,
    input_bf,
    normed_in,
    inv_in,
    first_grad,
    proj_weight,
    norm_gain,
):
    channels = gate_grad_bf.shape[2]
    sig_left = jax.nn.sigmoid(factor_pre[:channels])
    lin_left = factor_pre[channels : 2 * channels]
    sig_right = jax.nn.sigmoid(factor_pre[2 * channels : 3 * channels])
    lin_right = factor_pre[3 * channels :]
    masked_left = left_grad.astype(jnp.float32) * keep_both
    masked_right = right_grad.astype(jnp.float32) * keep_both
    factor_grad = jnp.concatenate(
        [
            masked_left * lin_left * sig_left * (1.0 - sig_left),
            masked_left * sig_left,
            masked_right * lin_right * sig_right * (1.0 - sig_right),
            masked_right * sig_right,
        ],
        axis=0,
    ).astype(jnp.bfloat16)
    grad_proj = jnp.concatenate(
        [
            contract("rld,erl->de", input_bf, factor_grad),
            contract("rld,rle->de", input_bf, gate_grad_bf),
        ],
        axis=1,
    )
    input_grad = contract("erl,de->rld", factor_grad, proj_weight[:, : 4 * channels]) + contract(
        "rle,de->rld", gate_grad_bf, proj_weight[:, 4 * channels :]
    )
    pair_grad, gain_in, bias_in = norm_backward(
        input_grad, normed_in, inv_in, norm_gain[0], 2, (0, 1)
    )
    return ((pair_grad + first_grad).astype(jnp.bfloat16), grad_proj, gain_in, bias_in)


def channel_products(left_part, right_part):
    return contract("acik,acjk->acij", left_part, right_part).astype(jnp.bfloat16)


def channel_grads(grad_part, left_part, right_part):
    left_grad = contract("acij,acjk->acik", grad_part, right_part).astype(jnp.bfloat16)
    right_grad = contract("acij,acik->acjk", grad_part, left_part).astype(jnp.bfloat16)
    return (left_grad, right_grad)


def local(
    pair, cotangent, lengths, proj_weight, out_weight, up_weight, down_weight, norm_gain, norm_bias
):
    pair_rows = pair[0]
    cot_rows = cotangent[0]
    rows_here, length_all, channels = pair_rows.shape
    groups = lax.axis_size("row")
    per_group = channels // groups
    first_row = lax.axis_index("row") * rows_here
    row_keep = (first_row + jnp.arange(rows_here, dtype=jnp.int32) < lengths[0]).astype(jnp.float32)
    col_keep = (jnp.arange(length_all, dtype=jnp.int32) < lengths[0]).astype(jnp.float32)
    entered = enter_rows(pair_rows, row_keep, col_keep, proj_weight, norm_gain, norm_bias)
    input_bf, normed_in, inv_in, factor_pre, gate_pre, keep_both, left_bf, right_bf = entered
    left_split = left_bf.reshape(groups, per_group, rows_here, length_all)
    right_split = right_bf.reshape(groups, per_group, rows_here, length_all)
    left_owned, right_owned = side_by_side((left_split, right_split), "row", 0, 2, 1)
    product_owned = channel_products(left_owned, right_owned)
    product_split = lax.all_to_all(product_owned, "row", split_axis=2, concat_axis=0, tiled=True)
    product_bf = product_split.reshape(channels, rows_here, length_all)
    middle = middle_rows(
        pair_rows,
        cot_rows,
        product_bf,
        gate_pre,
        out_weight,
        up_weight,
        down_weight,
        norm_gain,
        norm_bias,
    )
    (
        prod_grad_bf,
        first_grad,
        gate_grad_bf,
        grad_out,
        grad_up,
        grad_down,
        gain_prod,
        bias_prod,
        gain_tran,
        bias_tran,
    ) = middle
    summed_up, summed_down = together((grad_up, grad_down), ("crop", "row"))
    grad_split = prod_grad_bf.reshape(groups, per_group, rows_here, length_all)
    grad_owned = lax.all_to_all(grad_split, "row", split_axis=0, concat_axis=2, tiled=True)
    left_home, right_home = lax.all_to_all(
        for_sending(channel_grads(grad_owned, left_owned, right_owned)),
        "row",
        split_axis=2,
        concat_axis=0,
        tiled=True,
    )
    left_grad = left_home.reshape(channels, rows_here, length_all)
    right_grad = right_home.reshape(channels, rows_here, length_all)
    pair_grad, grad_proj, gain_in, bias_in = leave_rows(
        left_grad,
        right_grad,
        factor_pre,
        keep_both,
        gate_grad_bf,
        input_bf,
        normed_in,
        inv_in,
        first_grad,
        proj_weight,
        norm_gain,
    )
    gain_all = jnp.stack([gain_in, gain_prod, gain_tran])
    bias_all = jnp.stack([bias_in, bias_prod, bias_tran])
    summed_proj, summed_out, summed_gain, summed_bias = lax.psum(
        (grad_proj, grad_out, gain_all, bias_all), ("crop", "row")
    )
    factor = 1.0 / (rows_here * groups)
    return (
        pair_grad[None],
        summed_proj * factor,
        summed_out * factor,
        summed_up * factor,
        summed_down * factor,
        summed_gain * factor,
        summed_bias * factor,
    )


def solution(mesh):
    in_specs = (
        P("crop", "row", None, None),
        P("crop", "row", None, None),
        P("crop"),
        P(),
        P(),
        P(),
        P(),
        P(),
        P(),
    )
    out_specs = (P("crop", "row", None, None), P(), P(), P(), P(), P(), P())
    return jax.shard_map(local, mesh=mesh, in_specs=in_specs, out_specs=out_specs, check_vma=False)
```

profile of v0, /device:TPU:1, one launch (start us, length us, event | category | flops | bytes accessed | tf_op | source)
XLA Modules:
  0.0 557.1 jit_solution(11000184731263995300)
XLA Ops:
  17.9 3.2 pad_maximum_fusion.1
  22.3 62.7 %all_to_all.60 = bf16[64,4,8,512]{3,1,2,0:T(4,128)(2,1)S(1)} all-to-all(bf16[64,4,8,512]{3,1,2,0:T(4,128)(2,1)S(1)} %copy.100), channel_id=1, replica_groups=mesh['crop'=4,'row'=64] {'row'}, dimensions={0} | all-to-all | bytes 4194304 | tf_op jit(solution)/shard_map/all_to_all | solution.py:12
  89.7 5.9 %all-to-all-start.1 = ((bf16[1,2,512,512]{3,1,0,2:T(2,128)(2,1)}), bf16[1,2,512,512]{3,1,0,2:T(2,128)(2,1)S(1)}, u32[]{:S(2)}, u32[]{:S(2)}) async-start(bf16[1,2,512,512]{3,1,0,2:T(2,128)(2,1)} %copy.52), calls=%async_computation.1 | async-start | bytes 2097152 | tf_op jit(solution)/shard_map/all_to_all | solution.py:202
  96.9 27.0 %all-to-all-done.1 = bf16[1,2,512,512]{3,1,0,2:T(2,128)(2,1)S(1)} async-done(((bf16[1,2,512,512]{3,1,0,2:T(2,128)(2,1)}), bf16[1,2,512,512]{3,1,0,2:T(2,128)(2,1)S(1)}, u32[]{:S(2)}, u32[]{:S(2)}) %all-to-all-start.1) | async-done | bytes 1048608 | tf_op jit(solution)/shard_map/all_to_all | solution.py:202
  128.3 2.7 reshape.204
  132.4 2.5 convert_reduce_fusion
  137.3 3.4 multiply_convert_fusion.1
  140.8 3.2 fusion.81
  146.1 2.8 fusion.20
  149.0 4.7 multiply_convert_fusion.3
  158.1 2.3 reshape.200
  160.5 3.4 copy.62
  163.8 5.5 all-to-all-start.2
  169.4 3.3 convolution_bitcast_fusion.2
  172.7 2.4 reduce_sum.178
  175.1 22.4 %all-to-all-done.2 = bf16[64,2,8,512]{3,1,2,0:T(2,128)(2,1)} async-done(((bf16[64,2,8,512]{3,1,2,0:T(2,128)(2,1)}), bf16[64,2,8,512]{3,1,2,0:T(2,128)(2,1)}, u32[]{:S(2)}, u32[]{:S(2)}) %all-to-all-start.2) | async-done | bytes 1048608 | tf_op jit(solution)/shard_map/all_to_all | solution.py:229
  201.8 5.9 %all-to-all-start.3 = ((bf16[1,2,512,512]{3,1,0,2:T(2,128)(2,1)}), bf16[1,2,512,512]{3,1,0,2:T(2,128)(2,1)}, u32[]{:S(2)}, u32[]{:S(2)}) async-start(bf16[1,2,512,512]{3,1,0,2:T(2,128)(2,1)} %copy.64), calls=%async_computation.3 | async-start | bytes 2097152 | tf_op jit(solution)/shard_map/all_to_all | solution.py:230
  207.7 2.7 convolution_bitcast_fusion.4
  211.6 6.6 %convolution_bitcast_fusion = f32[65536]{0:T(1024)} fusion(f32[8,512,512]{2,1,0:T(8,128)} %copy-done.11, bf16[1,8,512,128]{3,2,1,0:T(8,128)(2,1)S(1)} %copy-done.21), kind=kOutput, calls=%fused_computation | convolution fusion | flops 547356672 | bytes 9699328 | tf_op jit(solution)/shard_map/rlh,rld->hd/dot_general | solution.py:30
  222.3 13.3 %all-to-all-done.3 = bf16[1,2,512,512]{3,1,0,2:T(2,128)(2,1)} async-done(((bf16[1,2,512,512]{3,1,0,2:T(2,128)(2,1)}), bf16[1,2,512,512]{3,1,0,2:T(2,128)(2,1)}, u32[]{:S(2)}, u32[]{:S(2)}) %all-to-all-start.3) | async-done | bytes 1048608 | tf_op jit(solution)/shard_map/all_to_all | solution.py:230
  235.7 5.5 all-to-all-start.4
  243.0 3.3 copy_bitcast_fusion.1
  246.3 3.9 reshape.205
  250.2 19.0 %all-to-all-done.4 = bf16[1,2,512,512]{3,1,0,2:T(2,128)(2,1)} async-done(((bf16[1,2,512,512]{3,1,0,2:T(2,128)(2,1)}), bf16[1,2,512,512]{3,1,0,2:T(2,128)(2,1)}, u32[]{:S(2)}, u32[]{:S(2)}) %all-to-all-start.4) | async-done | bytes 1048608 | tf_op jit(solution)/shard_map/all_to_all | solution.py:230
  269.2 3.3 copy_bitcast_fusion
  272.5 3.7 reshape.206
  276.2 5.6 %multiply_convert_fusion.7 = (bf16[128,8,512]{2,0,1:T(8,128)(2,1)S(1)}, bf16[128,8,512]{2,0,1:T(8,128)(2,1)S(1)}, bf16[128,8,512]{2,0,1:T(8,128)(2,1)S(1)}, bf16[128,8,512]{2,0,1:T(8,128)(2,1)S(1)}) fusion(f32[512,8,512]{2,0,1:T(8,128)} %copy-done.2, f32[128,8,512]{2,0,1:T(8,128)} %reshape.205, f32[8,512]{1,0:T(8,128)S(1)} %copy-done.31, ...), kind=kLoop, calls=%fused_computation.62 | loop fusion | flops 11534336 | bytes 16793600 | tf_op jit(solution)/shard_map/convert.11
  284.7 2.8 fusion.29
  289.0 4.7 fusion.47
  293.8 2.3 copy.81
  296.1 75.1 %all-reduce = (f32[3,128]{1,0:T(4,128)S(1)}, f32[3,128]{1,0:T(4,128)S(1)}) all-reduce(f32[3,128]{1,0:T(4,128)S(1)} %pad_maximum_fusion.6, f32[3,128]{1,0:T(4,128)S(1)} %pad_maximum_fusion.7), channel_id=1, replica_groups=mesh['crop'=4,'row'=64] {'crop','row'}, use_global_device_ids=true, to_apply=%region_18.0 | all-reduce | flops 768 | bytes 6144 | tf_op jit(solution)/shard_map/psum | solution.py:254
  372.3 172.0 %all-reduce.4.cloned.1.call-done = (f32[128,640]{1,0:T(8,128)}, f32[128,128]{1,0:T(8,128)}, f32[131072]{0:T(1024)}) async-done(((f32[128,640]{1,0:T(8,128)}, f32[128,128]{1,0:T(8,128)}, f32[131072]{0:T(1024)}), (f32[128,640]{1,0:T(8,128)}, f32[128,128]{1,0:T(8,128)}, f32[131072]{0:T(1024)})) %all-reduce.4.cloned.1.call-update) | async-done | bytes 917520 | tf_op jit(solution)/shard_map/psum | solution.py:254
  (158 shorter events, 54.3 us)
Async XLA Ops:
  7.2 128.7 %copy-start = (bf16[128,512]{1,0:T(8,128)(2,1)S(1)}, bf16[128,512]{1,0:T(8,128)(2,1)}, u32[]{:S(2)}) copy-start(bf16[128,512]{1,0:T(8,128)(2,1)} %param.14) | copy-start | bytes 393220
  9.6 122.7 %copy-start.22 = (f32[8,512]{1,0:T(8,128)}, f32[8,512]{1,0:T(8,128)S(1)}, u32[]{:S(2)}) copy-start(f32[8,512]{1,0:T(8,128)S(1)} %broadcast_multiply_fusion.11) | copy-start | bytes 49156
  10.0 122.3 %copy-start.26 = (f32[8,512]{1,0:T(8,128)}, f32[8,512]{1,0:T(8,128)S(1)}, u32[]{:S(2)}) copy-start(f32[8,512]{1,0:T(8,128)S(1)} %add_rsqrt_fusion.2) | copy-start | bytes 49156
  10.5 120.5 %copy-start.38 = (f32[128]{0:T(128)}, f32[128]{0:T(128)S(1)}, u32[]{:S(2)}) copy-start(f32[128]{0:T(128)S(1)} %get-tuple-element.61) | copy-start | bytes 1540
  10.5 121.8 %copy-start.36 = (f32[128]{0:T(128)}, f32[128]{0:T(128)S(1)}, u32[]{:S(2)}) copy-start(f32[128]{0:T(128)S(1)} %get-tuple-element.62) | copy-start | bytes 1540
  10.5 121.8 %copy-start.40 = (f32[128]{0:T(128)}, f32[128]{0:T(128)S(1)}, u32[]{:S(2)}) copy-start(f32[128]{0:T(128)S(1)} %get-tuple-element.54) | copy-start | bytes 1540
  12.0 3.2 copy-start.2
  87.5 8.0 %copy-start.19 = (bf16[1,8,512,128]{3,2,1,0:T(8,128)(2,1)S(1)}, bf16[1,8,512,128]{3,2,1,0:T(8,128)(2,1)}, u32[]{:S(2)}) copy-start(bf16[1,8,512,128]{3,2,1,0:T(8,128)(2,1)} %param.10) | copy-start | bytes 3145732
  89.7 34.2 %all-to-all-start.1 = ((bf16[1,2,512,512]{3,1,0,2:T(2,128)(2,1)}), bf16[1,2,512,512]{3,1,0,2:T(2,128)(2,1)S(1)}, u32[]{:S(2)}, u32[]{:S(2)}) async-start(bf16[1,2,512,512]{3,1,0,2:T(2,128)(2,1)} %copy.52), calls=%async_computation.1 | async-start | bytes 2097152 | tf_op jit(solution)/shard_map/all_to_all | solution.py:202
  132.3 3.5 copy-start.34
  132.4 3.5 copy-start.43
  135.2 34.1 %copy-start.24 = (f32[8,512]{1,0:T(8,128)}, f32[8,512]{1,0:T(8,128)S(1)}, u32[]{:S(2)}) copy-start(f32[8,512]{1,0:T(8,128)S(1)} %add_rsqrt_fusion) | copy-start | bytes 49156
  137.3 3.5 copy-start.11
  140.8 3.2 copy-start.13
  149.0 4.7 copy-start.4
  149.0 4.7 copy-start.39
  160.4 8.9 %copy-start.44 = (f32[128]{0:T(128)S(1)}, f32[128]{0:T(128)}, u32[]{:S(2)}) copy-start(f32[128]{0:T(128)} %get-tuple-element.53) | copy-start | bytes 1540
  163.8 33.6 %all-to-all-start.2 = ((bf16[64,2,8,512]{3,1,2,0:T(2,128)(2,1)}), bf16[64,2,8,512]{3,1,2,0:T(2,128)(2,1)}, u32[]{:S(2)}, u32[]{:S(2)}) async-start(bf16[64,2,8,512]{3,1,2,0:T(2,128)(2,1)} %copy.62), calls=%async_computation.2 | async-start | bytes 2097152 | tf_op jit(solution)/shard_map/all_to_all | solution.py:229
  201.8 8.6 %copy-start.23 = (f32[8,512]{1,0:T(8,128)S(1)}, f32[8,512]{1,0:T(8,128)}, u32[]{:S(2)}) copy-start(f32[8,512]{1,0:T(8,128)} %copy-done.22) | copy-start | bytes 49156
  201.8 8.6 %copy-start.27 = (f32[8,512]{1,0:T(8,128)S(1)}, f32[8,512]{1,0:T(8,128)}, u32[]{:S(2)}) copy-start(f32[8,512]{1,0:T(8,128)} %copy-done.26) | copy-start | bytes 49156
  201.8 8.6 %copy-start.37 = (f32[128]{0:T(128)S(1)}, f32[128]{0:T(128)}, u32[]{:S(2)}) copy-start(f32[128]{0:T(128)} %copy-done.36) | copy-start | bytes 1540
  201.8 8.6 %copy-start.41 = (f32[128]{0:T(128)S(1)}, f32[128]{0:T(128)}, u32[]{:S(2)}) copy-start(f32[128]{0:T(128)} %copy-done.40) | copy-start | bytes 1540
  201.8 33.9 %all-to-all-start.3 = ((bf16[1,2,512,512]{3,1,0,2:T(2,128)(2,1)}), bf16[1,2,512,512]{3,1,0,2:T(2,128)(2,1)}, u32[]{:S(2)}, u32[]{:S(2)}) async-start(bf16[1,2,512,512]{3,1,0,2:T(2,128)(2,1)} %copy.64), calls=%async_computation.3 | async-start | bytes 2097152 | tf_op jit(solution)/shard_map/all_to_all | solution.py:230
  211.6 6.6 %copy-start.18 = (bf16[1,4,64,8,512]{4,3,2,1,0:T(8,128)(2,1)S(1)}, bf16[1,4,64,8,512]{4,3,2,1,0:T(8,128)(2,1)}, u32[]{:S(2)}) copy-start(bf16[1,4,64,8,512]{4,3,2,1,0:T(8,128)(2,1)} %copy-done.17) | copy-start | bytes 6291460
  235.7 33.5 %all-to-all-start.4 = ((bf16[1,2,512,512]{3,1,0,2:T(2,128)(2,1)}), bf16[1,2,512,512]{3,1,0,2:T(2,128)(2,1)}, u32[]{:S(2)}, u32[]{:S(2)}) async-start(bf16[1,2,512,512]{3,1,0,2:T(2,128)(2,1)} %copy.67), calls=%async_computation.4 | async-start | bytes 2097152 | tf_op jit(solution)/shard_map/all_to_all | solution.py:230
  241.2 303.1 %all-reduce.4.cloned.1.call-start = ((), (), s32[]{:S(2)}) async-start(), calls=%async_computation.5 | async-start | bytes 1835008 | tf_op jit(solution)/shard_map/psum | solution.py:254
  272.5 3.7 copy-start.31
  284.7 4.3 copy-start.25
  289.0 4.8 copy-start.42
  289.0 4.7 copy-start.45
  289.0 4.7 copy-start.46
  293.7 256.3 %copy-start.1 = (bf16[128,512]{1,0:T(8,128)(2,1)S(1)}, bf16[128,512]{1,0:T(8,128)(2,1)}, u32[]{:S(2)}) copy-start(bf16[128,512]{1,0:T(8,128)(2,1)} %param.14) | copy-start | bytes 393220
  (23 other events, 43.0 us)
Sparse Core Ops, SparseCore 0:
  288.4 255.8 all-reduce.3
where the time goes:
time: 566 us; the launch traced here: 557 us
  waiting for transfers between devices  254 us (45%)
  blocking collectives  138 us (24%)
  other arithmetic  48.3 us (9%)
  local copies, waits for them, and re-layouts  41.2 us (7%)
  matrix products  37.6 us (7%)
  starting transfers between devices  22.8 us (4%)
  between operations  15.7 us (3%)
    psum x1, waiting for transfers between devices, local(): lax.psum((grad_proj, grad_out, gain_all, bias_all), ('crop', 'row'))  172 us
    psum x1, blocking collectives, local(): lax.psum((grad_proj, grad_out, gain_all, bias_all), ('crop', 'row'))  75.1 us
    all_to_all x1, blocking collectives, side_by_side(): lax.all_to_all(both, axis, split_axis=split_dim, concat_axis=concat_dim,...  62.7 us
    dot_general x17, matrix products, contract(): jnp.einsum(pattern, left_side, right_side, preferred_element_type=jnp.flo...  37.6 us
    all_to_all x2, waiting for transfers between devices, local(): lax.all_to_all(for_sending(channel_grads(grad_owned, left_owned, right_ow...  32.3 us
    all_to_all x1, waiting for transfers between devices, local(): lax.all_to_all(product_owned, 'row', split_axis=2, concat_axis=0, tiled=T...  27 us
    all_to_all x1, waiting for transfers between devices, local(): lax.all_to_all(grad_split, 'row', split_axis=0, concat_axis=2, tiled=True)  22.4 us
    unnamed x104, local copies, waits for them, and re-layouts  11.5 us
  transfers between devices with their start and end apart: 5, of which 5 were waited for; matrix products, arithmetic and copies ran while one was open for 7% of the time, Pallas kernels for 0%

commit v1 on v0

v1 whole, which is shorter than its diff:
```python
import functools

import jax
import jax.numpy as jnp
from jax import lax
from jax.experimental import pallas as pl
from jax.experimental.pallas import tpu as pltpu
from jax.sharding import PartitionSpec as P

EPSILON = 1e-05
F32 = jnp.float32
BF16 = jnp.bfloat16
MESH = pl.DeviceIdType.MESH
CHUNKS = 4


def place():
    crop = lax.axis_index("crop")
    row = lax.axis_index("row")
    core = lax.rem(crop, 2)
    zhi = lax.div(crop, 2)
    q = lax.div(row, 4)
    zlo = lax.rem(row, 4)
    return core, zhi * 4 + zlo, q


def device_at(core, z, q):
    return (lax.div(z, 4) * 2 + core, q * 4 + lax.rem(z, 4))


def send(src, dst, send_sem, recv_sem, device):
    return pltpu.make_async_remote_copy(
        src_ref=src,
        dst_ref=dst,
        send_sem=send_sem,
        recv_sem=recv_sem,
        device_id=device,
        device_id_type=MESH,
    )


def wait_for(ref, sem):
    pltpu.make_async_copy(ref, ref, sem).wait()


def signal(sem, device):
    pl.semaphore_signal(sem, inc=1, device_id=device, device_id_type=MESH)


def looped(count, body):
    lax.fori_loop(0, count, lambda i, carry: (body(i), carry)[1], 0)


def peers(body):
    crop = lax.axis_index("crop")
    row = lax.axis_index("row")
    q = lax.div(row, 4)
    z = lax.rem(row, 4)

    def step(i):
        n = i + 1
        dest = lax.rem(q + lax.rem(n, 16), 16) * 4 + lax.rem(z + lax.div(n, 16), 4)
        body(dest, (crop, dest))

    looped(63, step)


def sigmoid(x):
    return 0.5 + 0.5 * jnp.tanh(0.5 * x)


def dot(a, b, dim_a, dim_b):
    return lax.dot_general(a, b, (((dim_a,), (dim_b,)), ((), ())), preferred_element_type=F32)


def norm(values, axis):
    center = values - jnp.mean(values, axis=axis, keepdims=True)
    inv_std = lax.rsqrt(jnp.mean(center * center, axis=axis, keepdims=True) + EPSILON)
    return center * inv_std, inv_std


def norm_back(upstream, normed, inv_std, gain, axis):
    scaled = upstream * gain
    return inv_std * (
        scaled
        - jnp.mean(scaled, axis=axis, keepdims=True)
        - normed * jnp.mean(scaled * normed, axis=axis, keepdims=True)
    )


def to_flat(turn, value):
    turn[...] = value.reshape(1024, 128)
    return jnp.concatenate([turn[pl.ds(r, 128, stride=8), :] for r in range(8)], axis=1)


def to_rows(turn, value):
    for r in range(8):
        turn[pl.ds(r, 128, stride=8), :] = value[:, r * 128 : (r + 1) * 128]
    return turn[...].reshape(128, 8, 128)


def column(j):
    return pl.ds(pl.multiple_of(j * 128, 128), 128)


def whole_kernel(
    scale,
    pair_ref,
    cot_ref,
    keep_ref,
    wt_ref,
    wg_ref,
    out_ref,
    up_ref,
    down_ref,
    vec_ref,
    gain1_ref,
    bias1_ref,
    grad_ref,
    sums_ref,
    factors_out,
    factors_in,
    left_mat,
    right_mat,
    prod_out,
    prod_in,
    cots_out,
    cots_in,
    grads_out,
    grads_in,
    turn_a,
    turn_b,
    first_ref,
    gate_ref,
    acc,
    columns,
    from_core,
    from_plane,
    from_z,
    half,
    part,
    piece,
    all_z,
    all_plane,
    all_core,
    xs,
    xr,
    send_sems,
    recv_sems,
):
    core, z8, q = place()
    row = lax.axis_index("row")
    partner = device_at(1 - core, z8, q)
    barrier = pltpu.get_barrier_semaphore()
    signal(barrier, partner)
    peers(lambda dest, device: signal(barrier, device))
    looped(4, lambda i: signal(barrier, device_at(core, lax.rem(lax.div(z8, 4) * 4 + 4 + i, 8), q)))
    acc[...] = jnp.zeros_like(acc)
    columns[...] = jnp.zeros_like(columns)
    gain0, bias0 = vec_ref[0:1], vec_ref[1:2]
    gain2, bias2 = vec_ref[2:3], vec_ref[3:4]

    def rows_of(ref, j):
        return ref[:, column(j), :].reshape(1024, 128)

    def enter(j):
        normed, inv = norm(rows_of(pair_ref, j).astype(F32), 1)
        entered = (normed * gain0 + bias0).astype(BF16)
        return normed, inv, entered

    def enter_chunk(j):
        _, _, entered = enter(j)
        keep = keep_ref[j]
        pre = dot(wt_ref[...], entered, 1, 1)
        left = sigmoid(pre[0:128]) * pre[128:256] * keep
        right = sigmoid(pre[256:384]) * pre[384:512] * keep
        factors_out[:, 0, :, :, column(j)] = to_rows(turn_a, left).astype(BF16).reshape(64, 2, 8, 128)
        factors_out[:, 1, :, :, column(j)] = to_rows(turn_b, right).astype(BF16).reshape(64, 2, 8, 128)

    looped(CHUNKS, enter_chunk)
    pl.semaphore_wait(barrier, 68)

    def exchange(n, src, dst):
        def one(dest, device):
            send(src.at[dest], dst.at[row], xs.at[n], xr.at[n], device).start()

        peers(one)
        dst[row] = src[row]
        wait_for(dst.at[pl.ds(0, 63)], xr.at[n])

    exchange(0, factors_out, factors_in)

    def matrix(value):
        return value.astype(F32).reshape(512, 512).astype(BF16)

    def product(c):
        left_mat[c] = matrix(factors_in[:, 0, c])
        right_mat[c] = matrix(factors_in[:, 1, c])
        prod_out[:, c] = dot(left_mat[c], right_mat[c], 1, 1).reshape(64, 8, 512).astype(BF16)

    looped(2, product)
    exchange(1, prod_out, prod_in)

    def middle(j):
        flat = to_flat(turn_a, prod_in[:, :, :, column(j)].astype(F32))
        gain1 = gain1_ref[...]
        prod_normed, prod_inv = norm(flat, 0)
        prod_bf = (prod_normed * gain1 + bias1_ref[...]).astype(BF16)
        update = dot(prod_bf, out_ref[...], 0, 0)
        _, _, entered = enter(j)
        gate = sigmoid(dot(entered, wg_ref[...], 1, 0))
        first = (rows_of(pair_ref, j).astype(F32) + gate * update).astype(BF16)
        tran_normed, tran_inv = norm(first.astype(F32), 1)
        tran_bf = (tran_normed * gain2 + bias2).astype(BF16)
        cot = rows_of(cot_ref, j)
        tran_grad = jnp.zeros((1024, 128), F32)
        for h in range(2):
            at = slice(h * 256, (h + 1) * 256)
            hidden_pre = dot(tran_bf, up_ref[:, at], 1, 0)
            hidden_sig = sigmoid(hidden_pre)
            hidden = (hidden_pre * hidden_sig).astype(BF16)
            acc[h * 256 : (h + 1) * 256] += dot(hidden, cot, 0, 0)
            hidden_grad = (
                dot(cot, down_ref[at, :], 1, 1)
                * hidden_sig
                * (1.0 + hidden_pre * (1.0 - hidden_sig))
            ).astype(BF16)
            acc[512 + h * 256 : 512 + (h + 1) * 256] += dot(hidden_grad, tran_bf, 0, 0)
            tran_grad += dot(hidden_grad, up_ref[:, at], 1, 1)
        acc[1802:1803] += jnp.sum(tran_grad * tran_normed, axis=0, keepdims=True)
        acc[1805:1806] += jnp.sum(tran_grad, axis=0, keepdims=True)
        first_grad = norm_back(tran_grad, tran_normed, tran_inv, gain2, 1) + cot.astype(F32)
        update_grad = (first_grad * gate).astype(BF16)
        gate_grad = (first_grad * update * gate * (1.0 - gate)).astype(BF16)
        first_ref[:, column(j), :] = first_grad.reshape(8, 128, 128)
        gate_ref[:, column(j), :] = gate_grad.reshape(8, 128, 128)
        acc[1024:1152] += dot(prod_bf, update_grad, 1, 0)
        norm_grad = dot(out_ref[...], update_grad, 1, 1)
        columns[:, 0:1] += jnp.sum(norm_grad * prod_normed, axis=1, keepdims=True)
        columns[:, 1:2] += jnp.sum(norm_grad, axis=1, keepdims=True)
        prod_grad = norm_back(norm_grad, prod_normed, prod_inv, gain1, 0)
        cots_out[:, :, :, column(j)] = to_rows(turn_b, prod_grad).astype(BF16).reshape(64, 2, 8, 128)

    looped(CHUNKS, middle)
    exchange(2, cots_out, cots_in)

    def product_grads(c):
        grad = matrix(cots_in[:, c])
        grads_out[:, 0, c] = dot(grad, right_mat[c], 1, 0).reshape(64, 8, 512).astype(BF16)
        grads_out[:, 1, c] = dot(grad, left_mat[c], 0, 0).reshape(64, 8, 512).astype(BF16)

    looped(2, product_grads)
    exchange(3, grads_out, grads_in)

    def leave(j):
        normed, inv, entered = enter(j)
        keep = keep_ref[j]
        pre = dot(wt_ref[...], entered, 1, 1)
        left = to_flat(turn_a, grads_in[:, 0, :, :, column(j)].astype(F32)) * keep
        right = to_flat(turn_b, grads_in[:, 1, :, :, column(j)].astype(F32)) * keep
        left_sig = sigmoid(pre[0:128])
        right_sig = sigmoid(pre[256:384])
        factor_grad = jnp.concatenate(
            [
                (left * pre[128:256] * left_sig * (1.0 - left_sig)).astype(BF16),
                (left * left_sig).astype(BF16),
                (right * pre[384:512] * right_sig * (1.0 - right_sig)).astype(BF16),
                (right * right_sig).astype(BF16),
            ],
            axis=0,
        )
        gate_grad = rows_of(gate_ref, j)
        acc[1152:1664] += dot(factor_grad, entered, 1, 0)
        acc[1664:1792] += dot(gate_grad, entered, 0, 0)
        input_grad = dot(factor_grad, wt_ref[...], 0, 0) + dot(gate_grad, wg_ref[...], 1, 1)
        acc[1800:1801] += jnp.sum(input_grad * normed, axis=0, keepdims=True)
        acc[1803:1804] += jnp.sum(input_grad, axis=0, keepdims=True)
        result = norm_back(input_grad, normed, inv, gain0, 1) + rows_of(first_ref, j)
        grad_ref[:, column(j), :] = result.astype(BF16).reshape(8, 128, 128)

    looped(CHUNKS, leave)
    turned = columns[...].T
    acc[1801:1802] = turned[0:1]
    acc[1804:1805] = turned[1:2]

    def rows(i, count):
        return pl.ds(pl.multiple_of(i * count, count), count)

    first = send(acc.at[rows(1 - core, 1024)], from_core, send_sems.at[0], recv_sems.at[0], partner)
    first.start()
    first.wait_recv()
    half[...] = acc[rows(core, 1024)] + from_core[...]

    def to_plane(i):
        qd = lax.rem(q + i + 1, 16)
        send(half.at[rows(qd, 64)], from_plane.at[i], send_sems.at[1], recv_sems.at[1], device_at(core, z8, qd)).start()

    looped(15, to_plane)
    wait_for(from_plane, recv_sems.at[1])
    part[...] = half[rows(q, 64)] + jnp.sum(from_plane[...], axis=0)

    def to_z(i):
        zd = lax.rem(z8 + i + 1, 8)
        send(part.at[rows(zd, 8)], from_z.at[i], send_sems.at[2], recv_sems.at[2], device_at(core, zd, q)).start()

    looped(7, to_z)
    wait_for(from_z, recv_sems.at[2])
    piece[...] = (part[rows(z8, 8)] + jnp.sum(from_z[...], axis=0)) * scale

    def back_z(i):
        send(piece, all_z.at[rows(z8, 8)], send_sems.at[3], recv_sems.at[3], device_at(core, lax.rem(z8 + i + 1, 8), q)).start()

    looped(7, back_z)
    all_z[rows(z8, 8)] = piece[...]
    wait_for(from_z, recv_sems.at[3])

    def back_plane(i):
        send(all_z, all_plane.at[rows(q, 64)], send_sems.at[4], recv_sems.at[4], device_at(core, z8, lax.rem(q + i + 1, 16))).start()

    looped(15, back_plane)
    all_plane[rows(q, 64)] = all_z[...]
    wait_for(from_plane, recv_sems.at[4])
    last = send(all_plane, all_core, send_sems.at[5], recv_sems.at[5], partner)
    last.start()
    sums_ref[rows(core, 1024)] = all_plane[...]
    last.wait_recv()
    sums_ref[rows(1 - core, 1024)] = all_core[...]
    first.wait_send()
    wait_for(from_plane, send_sems.at[1])
    wait_for(from_z, send_sems.at[2])
    wait_for(from_z, send_sems.at[3])
    wait_for(from_plane, send_sems.at[4])
    last.wait_send()
    wait_for(factors_in.at[pl.ds(0, 63)], xs.at[0])
    wait_for(prod_in.at[pl.ds(0, 63)], xs.at[1])
    wait_for(cots_in.at[pl.ds(0, 63)], xs.at[2])
    wait_for(grads_in.at[pl.ds(0, 63)], xs.at[3])


def local(
    pair, cotangent, lengths, proj_weight, out_weight, up_weight, down_weight, norm_gain, norm_bias
):
    pair_rows = pair[0]
    cot_rows = cotangent[0]
    rows_here, length_all, channels = pair_rows.shape
    wide = 4 * channels
    first_row = lax.axis_index("row") * rows_here
    row_keep = (first_row + jnp.arange(rows_here, dtype=jnp.int32) < lengths[0]).astype(F32)
    col_keep = (jnp.arange(length_all, dtype=jnp.int32) < lengths[0]).astype(F32)
    keep = (row_keep[None, :, None] * col_keep.reshape(CHUNKS, 1, 128)).reshape(CHUNKS, 1, 1024)
    vec = jnp.concatenate(
        [norm_gain[0:1], norm_bias[0:1], norm_gain[2:3], norm_bias[2:3], jnp.zeros((4, channels), F32)]
    )
    vmem = pl.BlockSpec(memory_space=pltpu.VMEM)
    both = (64, 2, 2, 8, 512)
    single = (64, 2, 8, 512)
    pair_grad, sums = pl.pallas_call(
        functools.partial(whole_kernel, 1.0 / length_all),
        out_shape=(
            jax.ShapeDtypeStruct(pair_rows.shape, BF16),
            jax.ShapeDtypeStruct((2048, 128), F32),
        ),
        in_specs=[vmem] * 11,
        out_specs=(vmem, vmem),
        scratch_shapes=[
            pltpu.VMEM(both, BF16),
            pltpu.VMEM(both, BF16),
            pltpu.VMEM((2, 512, 512), BF16),
            pltpu.VMEM((2, 512, 512), BF16),
            pltpu.VMEM(single, BF16),
            pltpu.VMEM(single, BF16),
            pltpu.VMEM(single, BF16),
            pltpu.VMEM(single, BF16),
            pltpu.VMEM(both, BF16),
            pltpu.VMEM(both, BF16),
            pltpu.VMEM((1024, 128), F32),
            pltpu.VMEM((1024, 128), F32),
            pltpu.VMEM(pair_rows.shape, F32),
            pltpu.VMEM(pair_rows.shape, BF16),
            pltpu.VMEM((2048, 128), F32),
            pltpu.VMEM((128, 128), F32),
            pltpu.VMEM((1024, 128), F32),
            pltpu.VMEM((15, 64, 128), F32),
            pltpu.VMEM((7, 8, 128), F32),
            pltpu.VMEM((1024, 128), F32),
            pltpu.VMEM((64, 128), F32),
            pltpu.VMEM((8, 128), F32),
            pltpu.VMEM((64, 128), F32),
            pltpu.VMEM((1024, 128), F32),
            pltpu.VMEM((1024, 128), F32),
            pltpu.SemaphoreType.DMA((4,)),
            pltpu.SemaphoreType.DMA((4,)),
            pltpu.SemaphoreType.DMA((6,)),
            pltpu.SemaphoreType.DMA((6,)),
        ],
        compiler_params=pltpu.CompilerParams(
            collective_id=0, has_side_effects=True, vmem_limit_bytes=60 * 1024 * 1024
        ),
        name="whole",
    )(
        pair_rows,
        cot_rows,
        keep,
        proj_weight[:, :wide].T,
        proj_weight[:, wide:],
        out_weight,
        up_weight,
        down_weight,
        vec,
        norm_gain[1][:, None],
        norm_bias[1][:, None],
    )
    return (
        pair_grad[None],
        sums[1152:1792].T,
        sums[1024:1152],
        sums[512:1024].T,
        sums[0:512],
        sums[1800:1803],
        sums[1803:1806],
    )


def solution(mesh):
    in_specs = (
        P("crop", "row", None, None),
        P("crop", "row", None, None),
        P("crop"),
        P(),
        P(),
        P(),
        P(),
        P(),
        P(),
    )
    out_specs = (P("crop", "row", None, None), P(), P(), P(), P(), P(), P())
    return jax.shard_map(local, mesh=mesh, in_specs=in_specs, out_specs=out_specs, check_vma=False)
```

time: 566 us -> 227 us (0.40); the launches traced: 557 us -> 227 us
  waiting for transfers between devices: 254 us -> 0 us
  Pallas kernels: 0 us -> 211 us
  blocking collectives: 138 us -> 0 us
  other arithmetic: 48.3 us -> 0.63 us
  matrix products: 37.6 us -> 0 us
  local copies, waits for them, and re-layouts: 41.2 us -> 14.2 us
  starting transfers between devices: 22.8 us -> 0 us
  between operations: 15.7 us -> 1.34 us
    pallas_call x0 -> x1, Pallas kernels: none -> 211 us  [local(): pl.pallas_call(functools.partial(whole_kernel, 1.0 / length_all), out_sha...]
    psum x1 -> x0, waiting for transfers between devices: 172 us -> none  [local(): lax.psum((grad_proj, grad_out, gain_all, bias_all), ('crop', 'row'))]
    all_to_all x4 -> x0, waiting for transfers between devices: 81.7 us -> none  [the longest x2 32.3 us: local(): lax.all_to_all(for_sending(channel_grads(grad_owned, left_owned, right_ow...]
    psum x1 -> x0, blocking collectives: 75.1 us -> none  [local(): lax.psum((grad_proj, grad_out, gain_all, bias_all), ('crop', 'row'))]
    all_to_all x1 -> x0, blocking collectives: 62.7 us -> none  [side_by_side(): lax.all_to_all(both, axis, split_axis=split_dim, concat_axis=concat_dim,...]
    dot_general x17 -> x0, matrix products: 37.6 us -> none  [contract(): jnp.einsum(pattern, left_side, right_side, preferred_element_type=jnp.flo...]
    all_to_all x4 -> x0, starting transfers between devices: 22.8 us -> none  [the longest x2 11.4 us: local(): lax.all_to_all(for_sending(channel_grads(grad_owned, left_owned, right_ow...]
    convert_element_type x8 -> x1, other arithmetic: 17 us -> 0.01 us  [local(): (jnp.arange(length_all, dtype=jnp.int32) < lengths[0]).astype(F32)]
  transfers between devices with their start and end apart: 5 -> 0, of which waited for: 5 -> 0; matrix products, arithmetic and copies ran while one was open for 7% -> 0% of each run, Pallas kernels for 0% -> 0%
where the time goes in v1:
time: 227 us
  Pallas kernels  211 us (93%)
  local copies, waits for them, and re-layouts  14.2 us (6%)
    pallas_call x1, Pallas kernels, local(): pl.pallas_call(functools.partial(whole_kernel, 1.0 / length_all), out_sha...  211 us

profile of v1, /device:TPU:1, one launch (start us, length us, event | category | flops | bytes accessed | tf_op | source)
XLA Modules:
  0.0 226.8 jit_solution(2599155872034936756)
XLA Ops:
  1.3 0.0 copy-start.1
  1.3 0.0 copy-start.2
  1.3 0.6 copy-done.1
  2.0 0.0 copy-done.2
  2.0 0.6 concatenate.3.vec_ref
  2.6 0.1 broadcast_bitcast_fusion
  2.7 0.6 broadcast_multiply_fusion.keep_ref
  3.3 1.4 slice.43.wg_ref
  4.7 0.7 copy.18.bias1_ref
  5.4 0.7 copy.17.gain1_ref
  6.2 0.0 slice-start
  6.2 0.9 slice-done
  7.1 0.8 copy.21
  7.8 210.6 %whole.1 = (bf16[8,512,128]{2,1,0:T(8,128)(2,1)}, f32[2048,128]{1,0:T(8,128)}) custom-call(bf16[8,512,128]{2,1,0:T(8,128)(2,1)} %bitcast.18, bf16[8,512,128]{2,1,0:T(8,128)(2,1)} %bitcast.19, f32[4,1,1024]{2,1,0:T(1,128)} %broadcast_multiply_fusion.keep_ref, bf16[512,128]{1,0:T(8,128)(2,1)} %bitcast.21, bf16[128,128]{1,0:T(8,128)(2,1)} %slice.43.wg_ref, ...), custom_call_target="tpu_custom_call" | custom-call | tf_op jit(solution)/shard_map/whole/pallas_call | solution.py:357
  218.4 1.3 fusion.1
  219.8 1.5 slice.51
  221.3 1.0 slice_bitcast_fusion
  222.3 0.0 copy-start
  222.3 1.9 fusion.2
  224.1 0.9 copy.19
  225.0 0.8 copy.20
  225.8 0.0 copy-done
  225.8 1.0 copy.24
  (5 shorter events, 0.0 us)
Async XLA Ops:
  1.3 0.7 copy-start.1
  1.3 0.7 copy-start.2
  6.2 0.9 slice-start
  222.3 3.6 %copy-start = (bf16[8,512,128]{2,1,0:T(8,128)(2,1)S(1)}, bf16[8,512,128]{2,1,0:T(8,128)(2,1)}, u32[]{:S(2)}) copy-start(bf16[8,512,128]{2,1,0:T(8,128)(2,1)} %get-tuple-element.9) | copy-start | bytes 3145732

commit v2 on v1

v2 whole, which is shorter than its diff:
```python
import functools

import jax
import jax.numpy as jnp
from jax import lax
from jax.experimental import pallas as pl
from jax.experimental.pallas import tpu as pltpu
from jax.sharding import PartitionSpec as P

EPSILON = 1e-05
F32 = jnp.float32
BF16 = jnp.bfloat16
MESH = pl.DeviceIdType.MESH
CHUNKS = 4


def place():
    crop = lax.axis_index("crop")
    row = lax.axis_index("row")
    core = lax.rem(crop, 2)
    zhi = lax.div(crop, 2)
    q = lax.div(row, 4)
    zlo = lax.rem(row, 4)
    return core, zhi * 4 + zlo, q


def device_at(core, z, q):
    return (lax.div(z, 4) * 2 + core, q * 4 + lax.rem(z, 4))


def send(src, dst, send_sem, recv_sem, device):
    return pltpu.make_async_remote_copy(
        src_ref=src,
        dst_ref=dst,
        send_sem=send_sem,
        recv_sem=recv_sem,
        device_id=device,
        device_id_type=MESH,
    )


def wait_for(ref, sem):
    pltpu.make_async_copy(ref, ref, sem).wait()


def signal(sem, device):
    pl.semaphore_signal(sem, inc=1, device_id=device, device_id_type=MESH)


def looped(count, body):
    lax.fori_loop(0, count, lambda i, carry: (body(i), carry)[1], 0)


def peers(body):
    crop = lax.axis_index("crop")
    row = lax.axis_index("row")
    q = lax.div(row, 4)
    z = lax.rem(row, 4)

    def step(i):
        n = i + 1
        dest = lax.rem(q + lax.rem(n, 16), 16) * 4 + lax.rem(z + lax.div(n, 16), 4)
        body(dest, (crop, dest))

    looped(63, step)


def sigmoid(x):
    return 0.5 + 0.5 * jnp.tanh(0.5 * x)


def dot(a, b, dim_a, dim_b):
    return lax.dot_general(a, b, (((dim_a,), (dim_b,)), ((), ())), preferred_element_type=F32)


def norm(values, axis):
    center = values - jnp.mean(values, axis=axis, keepdims=True)
    inv_std = lax.rsqrt(jnp.mean(center * center, axis=axis, keepdims=True) + EPSILON)
    return center * inv_std, inv_std


def norm_back(upstream, normed, inv_std, gain, axis):
    scaled = upstream * gain
    return inv_std * (
        scaled
        - jnp.mean(scaled, axis=axis, keepdims=True)
        - normed * jnp.mean(scaled * normed, axis=axis, keepdims=True)
    )


def to_flat(turn, value):
    turn[...] = value.reshape(1024, 128)
    return jnp.concatenate([turn[pl.ds(r, 128, stride=8), :] for r in range(8)], axis=1)


def to_rows(turn, value):
    for r in range(8):
        turn[pl.ds(r, 128, stride=8), :] = value[:, r * 128 : (r + 1) * 128]
    return turn[...].reshape(128, 8, 128)


def column(j):
    return pl.ds(pl.multiple_of(j * 128, 128), 128)


def place_of(ref, j):
    return ref[:, column(j), :].reshape(1024, 128)


def rows(i, count):
    return pl.ds(pl.multiple_of(i * count, count), count)


def block(b):
    return slice(b * 128, (b + 1) * 128)


def whole_kernel(
    scale,
    lengths_ref,
    pair_ref,
    cot_ref,
    proj_ref,
    out_ref,
    up_ref,
    down_ref,
    gain_ref,
    bias_ref,
    grad_ref,
    sum_proj,
    sum_out,
    sum_up,
    sum_down,
    sum_gain,
    sum_bias,
    factors_out,
    factors_in,
    left_mat,
    right_mat,
    prod_out,
    prod_in,
    cots_out,
    cots_in,
    cot_mat,
    cot_turned,
    grads_out,
    grads_in,
    turn_a,
    turn_b,
    wt_ref,
    gain_col,
    bias_col,
    first_ref,
    gate_ref,
    acc,
    tail,
    columns,
    from_core,
    from_plane,
    from_z,
    half,
    part,
    piece,
    all_z,
    all_plane,
    all_core,
    acc_sum,
    tail_core,
    tail_half,
    tail_plane,
    tail_part,
    tail_z,
    tail_piece,
    tail_all,
    tail_other,
    xs,
    xr,
    send_sems,
    recv_sems,
):
    core, z8, q = place()
    row = lax.axis_index("row")
    partner = device_at(1 - core, z8, q)
    barrier = pltpu.get_barrier_semaphore()
    signal(barrier, partner)
    peers(lambda dest, device: signal(barrier, device))
    looped(4, lambda i: signal(barrier, device_at(core, lax.rem(lax.div(z8, 4) * 4 + 4 + i, 8), q)))
    acc[...] = jnp.zeros_like(acc)
    tail[...] = jnp.zeros_like(tail)
    columns[...] = jnp.zeros_like(columns)
    for b in range(4):
        wt_ref[block(b)] = proj_ref[:, block(b)].T
    gain_col[...] = jnp.broadcast_to(gain_ref[1:2], (128, 128)).T
    bias_col[...] = jnp.broadcast_to(bias_ref[1:2], (128, 128)).T
    gain0, bias0 = gain_ref[0:1], bias_ref[0:1]
    gain2, bias2 = gain_ref[2:3], bias_ref[2:3]
    gate_weight = slice(512, 640)

    def enter(j):
        normed, inv = norm(place_of(pair_ref, j).astype(F32), 1)
        entered = (normed * gain0 + bias0).astype(BF16)
        return normed, inv, entered

    def keep_of(j):
        at = lax.broadcasted_iota(jnp.int32, (1, 1024), 1)
        row_at = row * 8 + lax.shift_right_logical(at, 7)
        col_at = j * 128 + jnp.bitwise_and(at, 127)
        return jnp.where(jnp.maximum(row_at, col_at) < lengths_ref[0], 1.0, 0.0)

    def start_chunk(n, j, src, dst):
        def one(dest, device):
            send(src.at[j, dest], dst.at[j, row], xs.at[n, j], xr.at[n, j], device).start()

        peers(one)
        dst[j, row] = src[j, row]

    def wait_chunk(n, j, dst):
        wait_for(dst.at[j, pl.ds(0, 63)], xr.at[n, j])

    def enter_chunk(j):
        _, _, entered = enter(j)
        keep = keep_of(j)
        pre = dot(wt_ref[...], entered, 1, 1)
        left = sigmoid(pre[0:128]) * pre[128:256] * keep
        right = sigmoid(pre[256:384]) * pre[384:512] * keep
        factors_out[j, :, 0] = to_rows(turn_a, left).astype(BF16).reshape(64, 2, 8, 128)
        factors_out[j, :, 1] = to_rows(turn_b, right).astype(BF16).reshape(64, 2, 8, 128)

        @pl.when(j == 0)
        def _():
            pl.semaphore_wait(barrier, 68)

        start_chunk(0, j, factors_out, factors_in)

    looped(CHUNKS, enter_chunk)

    def matrix(value):
        return value.astype(F32).reshape(512, 128)

    def gather_factors(j):
        wait_chunk(0, j, factors_in)
        for c in range(2):
            left_mat[c, :, column(j)] = matrix(factors_in[j, :, 0, c]).astype(BF16)
            right_mat[c, :, column(j)] = matrix(factors_in[j, :, 1, c]).astype(BF16)

    looped(CHUNKS, gather_factors)

    def product(j):
        for c in range(2):
            prod = dot(left_mat[c], right_mat[c, rows(j, 128), :], 1, 1)
            prod_out[j, :, c] = prod.reshape(64, 8, 128).astype(BF16)
        start_chunk(1, j, prod_out, prod_in)

    looped(CHUNKS, product)

    def middle(j):
        _, _, entered = enter(j)
        gate = sigmoid(dot(entered, proj_ref[:, gate_weight], 1, 0))
        cot = place_of(cot_ref, j)
        cot_t = cot.T
        wait_chunk(1, j, prod_in)
        flat = to_flat(turn_a, prod_in[j].astype(F32))
        gain1 = gain_col[:, 0:1]
        prod_normed, prod_inv = norm(flat, 0)
        prod_bf = (prod_normed * gain1 + bias_col[:, 0:1]).astype(BF16)
        update = dot(prod_bf, out_ref[...], 0, 0)
        first = (place_of(pair_ref, j).astype(F32) + gate * update).astype(BF16)
        tran_normed, tran_inv = norm(first.astype(F32), 1)
        tran_bf = (tran_normed * gain2 + bias2).astype(BF16)
        tran_t = tran_bf.T
        tran_grad = jnp.zeros((1024, 128), F32)
        for h in range(2):
            at = slice(h * 256, (h + 1) * 256)
            hidden_pre = dot(tran_bf, up_ref[:, at], 1, 0)
            hidden_sig = sigmoid(hidden_pre)
            hidden = (hidden_pre * hidden_sig).astype(BF16)
            down_term = dot(cot_t, hidden, 1, 0)
            hidden_grad = (
                dot(cot, down_ref[at, :], 1, 1)
                * hidden_sig
                * (1.0 + hidden_pre * (1.0 - hidden_sig))
            ).astype(BF16)
            up_term = dot(tran_t, hidden_grad, 1, 0)
            for k in range(2):
                acc[block(2 * h + k)] += down_term[:, block(k)]
                acc[block(4 + 2 * h + k)] += up_term[:, block(k)]
            tran_grad += dot(hidden_grad, up_ref[:, at], 1, 1)
        acc[1282:1283] += jnp.sum(tran_grad * tran_normed, axis=0, keepdims=True)
        acc[1285:1286] += jnp.sum(tran_grad, axis=0, keepdims=True)
        first_grad = norm_back(tran_grad, tran_normed, tran_inv, gain2, 1) + cot.astype(F32)
        update_grad = (first_grad * gate).astype(BF16)
        gate_grad = (first_grad * update * gate * (1.0 - gate)).astype(BF16)
        acc[block(8)] += dot(prod_bf, update_grad, 1, 0)
        norm_grad = dot(out_ref[...], update_grad, 1, 1)
        columns[:, 0:1] += jnp.sum(norm_grad * prod_normed, axis=1, keepdims=True)
        columns[:, 1:2] += jnp.sum(norm_grad, axis=1, keepdims=True)
        prod_grad = norm_back(norm_grad, prod_normed, prod_inv, gain1, 0)
        cots_out[j] = to_rows(turn_b, prod_grad).astype(BF16).reshape(64, 2, 8, 128)
        start_chunk(2, j, cots_out, cots_in)
        first_ref[:, column(j), :] = first_grad.reshape(8, 128, 128)
        gate_ref[:, column(j), :] = dot(gate_grad, proj_ref[:, gate_weight], 1, 1).reshape(8, 128, 128)
        acc[block(9)] += dot(entered.T, gate_grad, 1, 0)

    looped(CHUNKS, middle)
    for b in range(4):
        acc[block(b)] = acc[block(b)].T
    turned = columns[...].T
    acc[1281:1282] = turned[0:1]
    acc[1284:1285] = turned[1:2]

    first = send(acc.at[rows(1 - core, 1024)], from_core, send_sems.at[0], recv_sems.at[0], partner)
    first.start()
    first.wait_recv()
    half[...] = acc[rows(core, 1024)] + from_core[...]

    def to_plane(i):
        qd = lax.rem(q + i + 1, 16)
        send(half.at[rows(qd, 64)], from_plane.at[i], send_sems.at[1], recv_sems.at[1], device_at(core, z8, qd)).start()

    looped(15, to_plane)

    def gather_cots(j):
        wait_chunk(2, j, cots_in)
        for c in range(2):
            grad = matrix(cots_in[j, :, c])
            cot_mat[c, :, column(j)] = grad.astype(BF16)
            cot_turned[c, rows(j, 128), :] = grad.T.astype(BF16)

    looped(CHUNKS, gather_cots)
    wait_for(from_plane, recv_sems.at[1])
    part[...] = half[rows(q, 64)] + jnp.sum(from_plane[...], axis=0)

    def to_z(i):
        zd = lax.rem(z8 + i + 1, 8)
        send(part.at[rows(zd, 8)], from_z.at[i], send_sems.at[2], recv_sems.at[2], device_at(core, zd, q)).start()

    looped(7, to_z)

    def product_grads(j):
        for c in range(2):
            left = dot(cot_mat[c], right_mat[c, :, column(j)], 1, 0)
            right = dot(cot_turned[c], left_mat[c, :, column(j)], 1, 0)
            grads_out[j, :, 0, c] = left.reshape(64, 8, 128).astype(BF16)
            grads_out[j, :, 1, c] = right.reshape(64, 8, 128).astype(BF16)
        start_chunk(3, j, grads_out, grads_in)

    looped(CHUNKS, product_grads)
    wait_for(from_z, recv_sems.at[2])
    piece[...] = (part[rows(z8, 8)] + jnp.sum(from_z[...], axis=0)) * scale

    def back_z(i):
        send(piece, all_z.at[rows(z8, 8)], send_sems.at[3], recv_sems.at[3], device_at(core, lax.rem(z8 + i + 1, 8), q)).start()

    looped(7, back_z)
    all_z[rows(z8, 8)] = piece[...]

    def leave(j):
        normed, inv, entered = enter(j)
        keep = keep_of(j)
        pre = dot(wt_ref[...], entered, 1, 1)
        left_sig = sigmoid(pre[0:128])
        right_sig = sigmoid(pre[256:384])
        wait_chunk(3, j, grads_in)
        left = to_flat(turn_a, grads_in[j, :, 0].astype(F32)) * keep
        right = to_flat(turn_b, grads_in[j, :, 1].astype(F32)) * keep
        factor_grad = jnp.concatenate(
            [
                (left * pre[128:256] * left_sig * (1.0 - left_sig)).astype(BF16),
                (left * left_sig).astype(BF16),
                (right * pre[384:512] * right_sig * (1.0 - right_sig)).astype(BF16),
                (right * right_sig).astype(BF16),
            ],
            axis=0,
        )
        terms = dot(factor_grad, entered, 1, 0)
        for core_half in range(2):
            for b in range(16):
                at = core_half * 256 + b * 16
                to = core_half * 384 + b * 24
                tail[to : to + 16] += terms[at : at + 16]
        input_grad = dot(factor_grad, wt_ref[...], 0, 0) + place_of(gate_ref, j)
        tail[16:17] += jnp.sum(input_grad * normed, axis=0, keepdims=True)
        tail[17:18] += jnp.sum(input_grad, axis=0, keepdims=True)
        result = norm_back(input_grad, normed, inv, gain0, 1) + place_of(first_ref, j)
        grad_ref[:, column(j), :] = result.astype(BF16).reshape(8, 128, 128)

    looped(CHUNKS, leave)

    tail_first = send(tail.at[rows(1 - core, 384)], tail_core, send_sems.at[6], recv_sems.at[6], partner)
    tail_first.start()
    tail_first.wait_recv()
    tail_half[...] = tail[rows(core, 384)] + tail_core[...]

    def tail_to_plane(i):
        qd = lax.rem(q + i + 1, 16)
        send(tail_half.at[rows(qd, 24)], tail_plane.at[i], send_sems.at[7], recv_sems.at[7], device_at(core, z8, qd)).start()

    looped(15, tail_to_plane)
    wait_for(from_z, recv_sems.at[3])

    def back_plane(i):
        send(all_z, all_plane.at[rows(q, 64)], send_sems.at[4], recv_sems.at[4], device_at(core, z8, lax.rem(q + i + 1, 16))).start()

    looped(15, back_plane)
    all_plane[rows(q, 64)] = all_z[...]
    wait_for(tail_plane, recv_sems.at[7])
    tail_part[...] = (tail_half[rows(q, 24)] + jnp.sum(tail_plane[...], axis=0)) * scale

    def tail_to_z(i):
        zd = lax.rem(z8 + i + 1, 8)
        send(tail_part, tail_z.at[z8], send_sems.at[8], recv_sems.at[8], device_at(core, zd, q)).start()

    looped(7, tail_to_z)
    tail_z[z8] = tail_part[...]
    wait_for(from_plane, recv_sems.at[4])
    last = send(all_plane, all_core, send_sems.at[5], recv_sems.at[5], partner)
    last.start()
    wait_for(tail_z.at[pl.ds(0, 7)], recv_sems.at[8])
    tail_piece[...] = jnp.sum(tail_z[...], axis=0)

    def tail_back(i):
        send(tail_piece, tail_all.at[rows(q, 24)], send_sems.at[9], recv_sems.at[9], device_at(core, z8, lax.rem(q + i + 1, 16))).start()

    looped(15, tail_back)
    tail_all[rows(q, 24)] = tail_piece[...]
    last.wait_recv()
    acc_sum[rows(core, 1024)] = all_plane[...]
    acc_sum[rows(1 - core, 1024)] = all_core[...]
    for b in range(4):
        sum_down[block(b)] = acc_sum[block(b)]
        sum_up[:, block(b)] = acc_sum[block(4 + b)]
    sum_out[...] = acc_sum[block(8)]
    sum_proj[:, gate_weight] = acc_sum[block(9)]
    sum_gain[1:3] = acc_sum[1281:1283]
    sum_bias[1:3] = acc_sum[1284:1286]
    wait_for(tail_plane, recv_sems.at[9])
    tail_last = send(tail_all, tail_other, send_sems.at[10], recv_sems.at[10], partner)
    tail_last.start()

    def put_proj(which, source):
        for k in range(2):
            terms = jnp.concatenate([source[b * 24 : b * 24 + 16] for b in range(8 * k, 8 * k + 8)], axis=0)
            sum_proj[:, column(which * 2 + k)] = terms.T

    put_proj(core, tail_all)
    tail_last.wait_recv()
    put_proj(1 - core, tail_other)
    norm_terms = jnp.where(core == 0, tail_all[16:24], tail_other[16:24])
    sum_gain[0:1] = norm_terms[0:1]
    sum_bias[0:1] = norm_terms[1:2]

    first.wait_send()
    wait_for(from_plane, send_sems.at[1])
    wait_for(from_z, send_sems.at[2])
    wait_for(from_z, send_sems.at[3])
    wait_for(from_plane, send_sems.at[4])
    last.wait_send()
    tail_first.wait_send()
    wait_for(tail_plane, send_sems.at[7])
    wait_for(tail_z.at[pl.ds(0, 7)], send_sems.at[8])
    wait_for(tail_plane, send_sems.at[9])
    tail_last.wait_send()

    def settle(j):
        wait_for(factors_in.at[j, pl.ds(0, 63)], xs.at[0, j])
        wait_for(prod_in.at[j, pl.ds(0, 63)], xs.at[1, j])
        wait_for(cots_in.at[j, pl.ds(0, 63)], xs.at[2, j])
        wait_for(grads_in.at[j, pl.ds(0, 63)], xs.at[3, j])

    looped(CHUNKS, settle)


def local(
    pair, cotangent, lengths, proj_weight, out_weight, up_weight, down_weight, norm_gain, norm_bias
):
    pair_rows = pair[0]
    cot_rows = cotangent[0]
    vmem = pl.BlockSpec(memory_space=pltpu.VMEM)
    both = (CHUNKS, 64, 2, 2, 8, 128)
    single = (CHUNKS, 64, 2, 8, 128)
    outs = pl.pallas_call(
        functools.partial(whole_kernel, 1.0 / pair_rows.shape[1]),
        out_shape=(
            jax.ShapeDtypeStruct(pair_rows.shape, BF16),
            jax.ShapeDtypeStruct(proj_weight.shape, F32),
            jax.ShapeDtypeStruct(out_weight.shape, F32),
            jax.ShapeDtypeStruct(up_weight.shape, F32),
            jax.ShapeDtypeStruct(down_weight.shape, F32),
            jax.ShapeDtypeStruct(norm_gain.shape, F32),
            jax.ShapeDtypeStruct(norm_bias.shape, F32),
        ),
        in_specs=[pl.BlockSpec(memory_space=pltpu.SMEM)] + [vmem] * 8,
        out_specs=(vmem,) * 7,
        scratch_shapes=[
            pltpu.VMEM(both, BF16),
            pltpu.VMEM(both, BF16),
            pltpu.VMEM((2, 512, 512), BF16),
            pltpu.VMEM((2, 512, 512), BF16),
            pltpu.VMEM(single, BF16),
            pltpu.VMEM(single, BF16),
            pltpu.VMEM(single, BF16),
            pltpu.VMEM(single, BF16),
            pltpu.VMEM((2, 512, 512), BF16),
            pltpu.VMEM((2, 512, 512), BF16),
            pltpu.VMEM(both, BF16),
            pltpu.VMEM(both, BF16),
            pltpu.VMEM((1024, 128), F32),
            pltpu.VMEM((1024, 128), F32),
            pltpu.VMEM((512, 128), BF16),
            pltpu.VMEM((128, 128), F32),
            pltpu.VMEM((128, 128), F32),
            pltpu.VMEM(pair_rows.shape, F32),
            pltpu.VMEM(pair_rows.shape, F32),
            pltpu.VMEM((2048, 128), F32),
            pltpu.VMEM((768, 128), F32),
            pltpu.VMEM((128, 128), F32),
            pltpu.VMEM((1024, 128), F32),
            pltpu.VMEM((15, 64, 128), F32),
            pltpu.VMEM((7, 8, 128), F32),
            pltpu.VMEM((1024, 128), F32),
            pltpu.VMEM((64, 128), F32),
            pltpu.VMEM((8, 128), F32),
            pltpu.VMEM((64, 128), F32),
            pltpu.VMEM((1024, 128), F32),
            pltpu.VMEM((1024, 128), F32),
            pltpu.VMEM((2048, 128), F32),
            pltpu.VMEM((384, 128), F32),
            pltpu.VMEM((384, 128), F32),
            pltpu.VMEM((15, 24, 128), F32),
            pltpu.VMEM((24, 128), F32),
            pltpu.VMEM((8, 24, 128), F32),
            pltpu.VMEM((24, 128), F32),
            pltpu.VMEM((384, 128), F32),
            pltpu.VMEM((384, 128), F32),
            pltpu.SemaphoreType.DMA((4, CHUNKS)),
            pltpu.SemaphoreType.DMA((4, CHUNKS)),
            pltpu.SemaphoreType.DMA((11,)),
            pltpu.SemaphoreType.DMA((11,)),
        ],
        compiler_params=pltpu.CompilerParams(
            collective_id=0, has_side_effects=True, vmem_limit_bytes=60 * 1024 * 1024
        ),
        name="whole",
    )(
        lengths,
        pair_rows,
        cot_rows,
        proj_weight,
        out_weight,
        up_weight,
        down_weight,
        norm_gain,
        norm_bias,
    )
    return (outs[0][None], *outs[1:])


def solution(mesh):
    in_specs = (
        P("crop", "row", None, None),
        P("crop", "row", None, None),
        P("crop"),
        P(),
        P(),
        P(),
        P(),
        P(),
        P(),
    )
    out_specs = (P("crop", "row", None, None), P(), P(), P(), P(), P(), P())
    return jax.shard_map(local, mesh=mesh, in_specs=in_specs, out_specs=out_specs, check_vma=False)
```

time: 227 us -> 193 us (0.85)
  Pallas kernels: 211 us -> 185 us
  local copies, waits for them, and re-layouts: 14.2 us -> 6.82 us
    pallas_call x1, Pallas kernels: 211 us -> 185 us  [local(): pl.pallas_call(functools.partial(whole_kernel, 1.0 / pair_rows.shape[1]),...]
    slice x6 -> x0, local copies, waits for them, and re-layouts: 6.94 us -> none  [the longest x1 1.85 us: local(): sums[0:512]]
    unnamed x10 -> x19, local copies, waits for them, and re-layouts: 4.13 us -> 6.82 us
where the time goes in v2:
time: 193 us
  Pallas kernels  185 us (96%)
  local copies, waits for them, and re-layouts  6.82 us (4%)
    pallas_call x1, Pallas kernels, local(): pl.pallas_call(functools.partial(whole_kernel, 1.0 / pair_rows.shape[1]),...  185 us
    unnamed x19, local copies, waits for them, and re-layouts  6.82 us

profile of v2, /device:TPU:1, one launch (start us, length us, event | category | flops | bytes accessed | tf_op | source)
XLA Modules:
  0.0 192.8 jit_solution(11885767720749510513)
XLA Ops:
  1.3 184.7 %whole.1 = (bf16[8,512,128]{2,1,0:T(8,128)(2,1)}, f32[128,640]{1,0:T(8,128)}, f32[128,128]{1,0:T(8,128)}, f32[128,512]{1,0:T(8,128)}, f32[512,128]{1,0:T(8,128)}, /*index=5*/f32[3,128]{1,0:T(4,128)}, f32[3,128]{1,0:T(4,128)}) custom-call(s32[1]{0:T(128)S(6)} %copy.23.lengths_ref, bf16[8,512,128]{2,1,0:T(8,128)(2,1)} %bitcast.3, ...), custom_call_target="tpu_custom_call" | custom-call | tf_op jit(solution)/shard_map/whole/pallas_call | solution.py:481
  186.0 0.0 copy-start
  186.0 2.3 %copy.24 = bf16[1,8,512,128]{3,2,1,0:T(8,128)(2,1)} copy(bf16[1,8,512,128]{3,2,1,0:T(8,128)(2,1)} %bitcast.5) | data formatting | bytes 2097152
  188.3 0.0 copy-done
  188.3 0.0 copy-start.3
  188.3 0.0 copy-start.2
  188.3 0.7 copy.25
  189.0 0.1 copy-done.3
  189.2 0.6 copy.26
  189.8 0.0 copy-done.2
  189.8 0.0 copy-start.1
  189.8 0.7 copy.27
  190.5 0.3 copy-done.1
  190.9 0.0 copy-start.5
  190.9 0.7 copy.28
  191.6 0.0 copy-done.5
  191.6 0.0 copy-start.4
  191.6 0.6 copy.29
  192.1 0.1 copy-done.4
  192.2 0.6 copy.30
Async XLA Ops:
  186.0 2.3 %copy-start = (f32[128,640]{1,0:T(8,128)S(1)}, f32[128,640]{1,0:T(8,128)}, u32[]{:S(2)}) copy-start(f32[128,640]{1,0:T(8,128)} %get-tuple-element.29) | copy-start | bytes 983044
  188.3 0.9 copy-start.3
  188.3 1.5 copy-start.2
  189.8 1.0 copy-start.1
  190.9 0.7 copy-start.5
  191.6 0.7 copy-start.4

commit v3 on v2

--- a/solution.py
+++ b/solution.py
@@ -59,8 +59,9 @@
 
     def step(i):
         n = i + 1
-        dest = lax.rem(q + lax.rem(n, 16), 16) * 4 + lax.rem(z + lax.div(n, 16), 4)
-        body(dest, (crop, dest))
+        qd = lax.rem(q + lax.rem(n, 16), 16)
+        zd = lax.rem(z + lax.div(n, 16), 4)
+        body(qd * 4 + zd, zd * 16 + qd, lax.div(n, 16), (crop, qd * 4 + zd))
 
     looped(63, step)
 
@@ -173,6 +174,10 @@
     tail_piece,
     tail_all,
     tail_other,
+    entered_ref,
+    factor_ref,
+    plane_terms,
+    natural,
     xs,
     xr,
     send_sems,
@@ -183,7 +188,7 @@
     partner = device_at(1 - core, z8, q)
     barrier = pltpu.get_barrier_semaphore()
     signal(barrier, partner)
-    peers(lambda dest, device: signal(barrier, device))
+    peers(lambda dest, owner, hop, device: signal(barrier, device))
     looped(4, lambda i: signal(barrier, device_at(core, lax.rem(lax.div(z8, 4) * 4 + 4 + i, 8), q)))
     acc[...] = jnp.zeros_like(acc)
     tail[...] = jnp.zeros_like(tail)
@@ -207,12 +212,22 @@
         col_at = j * 128 + jnp.bitwise_and(at, 127)
         return jnp.where(jnp.maximum(row_at, col_at) < lengths_ref[0], 1.0, 0.0)
 
-    def start_chunk(n, j, src, dst):
-        def one(dest, device):
-            send(src.at[j, dest], dst.at[j, row], xs.at[n, j], xr.at[n, j], device).start()
+    zlo = lax.rem(row, 4)
+    mine = zlo * 16 + q
+
+    def start_products(j):
+        def one(dest, owner, hop, device):
+            send(prod_out.at[j, dest], prod_in.at[j, mine], xs.at[1, j], xr.at[1, j], device).start()
 
         peers(one)
-        dst[j, row] = src[j, row]
+        prod_in[j, mine] = prod_out[j, row]
+
+    def start_cots(j):
+        def one(dest, owner, hop, device):
+            send(cots_out.at[j, owner], cots_in.at[j, row], xs.at[2, j], xr.at[2, j], device).start()
+
+        peers(one)
+        cots_in[j, row] = cots_out[j, mine]
 
     def wait_chunk(n, j, dst):
         wait_for(dst.at[j, pl.ds(0, 63)], xr.at[n, j])
@@ -223,25 +238,26 @@
         pre = dot(wt_ref[...], entered, 1, 1)
         left = sigmoid(pre[0:128]) * pre[128:256] * keep
         right = sigmoid(pre[256:384]) * pre[384:512] * keep
-        factors_out[j, :, 0] = to_rows(turn_a, left).astype(BF16).reshape(64, 2, 8, 128)
-        factors_out[j, :, 1] = to_rows(turn_b, right).astype(BF16).reshape(64, 2, 8, 128)
-
-        @pl.when(j == 0)
-        def _():
-            pl.semaphore_wait(barrier, 68)
-
-        start_chunk(0, j, factors_out, factors_in)
+        factors_out[:, 0, :, :, column(j)] = to_rows(turn_a, left).astype(BF16).reshape(64, 2, 8, 128)
+        factors_out[:, 1, :, :, column(j)] = to_rows(turn_b, right).astype(BF16).reshape(64, 2, 8, 128)
 
     looped(CHUNKS, enter_chunk)
+    pl.semaphore_wait(barrier, 68)
+
+    def start_factors(dest, owner, hop, device):
+        send(factors_out.at[owner], factors_in.at[row], xs.at[0, 0], xr.at[0, 0], device).start()
+
+    peers(start_factors)
+    factors_in[row] = factors_out[mine]
+    wait_for(factors_in.at[pl.ds(0, 63)], xr.at[0, 0])
 
     def matrix(value):
         return value.astype(F32).reshape(512, 128)
 
     def gather_factors(j):
-        wait_chunk(0, j, factors_in)
         for c in range(2):
-            left_mat[c, :, column(j)] = matrix(factors_in[j, :, 0, c]).astype(BF16)
-            right_mat[c, :, column(j)] = matrix(factors_in[j, :, 1, c]).astype(BF16)
+            left_mat[c, :, column(j)] = matrix(factors_in[:, 0, c, :, column(j)]).astype(BF16)
+            right_mat[c, :, column(j)] = matrix(factors_in[:, 1, c, :, column(j)]).astype(BF16)
 
     looped(CHUNKS, gather_factors)
 
@@ -249,7 +265,7 @@
         for c in range(2):
             prod = dot(left_mat[c], right_mat[c, rows(j, 128), :], 1, 1)
             prod_out[j, :, c] = prod.reshape(64, 8, 128).astype(BF16)
-        start_chunk(1, j, prod_out, prod_in)
+        start_products(j)
 
     looped(CHUNKS, product)
 
@@ -296,7 +312,7 @@
         columns[:, 1:2] += jnp.sum(norm_grad, axis=1, keepdims=True)
         prod_grad = norm_back(norm_grad, prod_normed, prod_inv, gain1, 0)
         cots_out[j] = to_rows(turn_b, prod_grad).astype(BF16).reshape(64, 2, 8, 128)
-        start_chunk(2, j, cots_out, cots_in)
+        start_cots(j)
         first_ref[:, column(j), :] = first_grad.reshape(8, 128, 128)
         gate_ref[:, column(j), :] = dot(gate_grad, proj_ref[:, gate_weight], 1, 1).reshape(8, 128, 128)
         acc[block(9)] += dot(entered.T, gate_grad, 1, 0)
@@ -340,11 +356,16 @@
         for c in range(2):
             left = dot(cot_mat[c], right_mat[c, :, column(j)], 1, 0)
             right = dot(cot_turned[c], left_mat[c, :, column(j)], 1, 0)
-            grads_out[j, :, 0, c] = left.reshape(64, 8, 128).astype(BF16)
-            grads_out[j, :, 1, c] = right.reshape(64, 8, 128).astype(BF16)
-        start_chunk(3, j, grads_out, grads_in)
+            grads_out[:, 0, c, :, column(j)] = left.reshape(64, 8, 128).astype(BF16)
+            grads_out[:, 1, c, :, column(j)] = right.reshape(64, 8, 128).astype(BF16)
 
     looped(CHUNKS, product_grads)
+
+    def start_grads(dest, owner, hop, device):
+        send(grads_out.at[dest], grads_in.at[mine], xs.at[3, hop], xr.at[3, hop], device).start()
+
+    peers(start_grads)
+    grads_in[mine] = grads_out[row]
     wait_for(from_z, recv_sems.at[2])
     piece[...] = (part[rows(z8, 8)] + jnp.sum(from_z[...], axis=0)) * scale
 
@@ -354,37 +375,68 @@
     looped(7, back_z)
     all_z[rows(z8, 8)] = piece[...]
 
-    def leave(j):
-        normed, inv, entered = enter(j)
+    def prepare(j):
+        _, _, entered = enter(j)
         keep = keep_of(j)
         pre = dot(wt_ref[...], entered, 1, 1)
         left_sig = sigmoid(pre[0:128])
         right_sig = sigmoid(pre[256:384])
-        wait_chunk(3, j, grads_in)
-        left = to_flat(turn_a, grads_in[j, :, 0].astype(F32)) * keep
-        right = to_flat(turn_b, grads_in[j, :, 1].astype(F32)) * keep
-        factor_grad = jnp.concatenate(
-            [
-                (left * pre[128:256] * left_sig * (1.0 - left_sig)).astype(BF16),
-                (left * left_sig).astype(BF16),
-                (right * pre[384:512] * right_sig * (1.0 - right_sig)).astype(BF16),
-                (right * right_sig).astype(BF16),
-            ],
-            axis=0,
+        entered_ref[j] = entered
+        left_kept = left_sig * keep
+        right_kept = right_sig * keep
+        factor_ref[j, 0] = pre[128:256] * left_kept * (1.0 - left_sig)
+        factor_ref[j, 1] = left_kept
+        factor_ref[j, 2] = pre[384:512] * right_kept * (1.0 - right_sig)
+        factor_ref[j, 3] = right_kept
+
+    looped(CHUNKS, prepare)
+
+    def plane_flat(turn, value):
+        turn[0:256] = value.reshape(256, 128)
+        return jnp.concatenate([turn[pl.ds(r, 32, stride=8), :] for r in range(8)], axis=1)
+
+    def leave(hop, count):
+        zs = lax.rem(zlo + 4 - hop, 4)
+        wait_for(grads_in.at[pl.ds(0, count)], xr.at[3, hop])
+        plane = rows(zs, 16)
+        own = rows(zs, 32)
+        weights = jnp.concatenate(
+            [wt_ref[pl.ds(pl.multiple_of(b * 128 + zs * 32, 32), 32), :] for b in range(4)], axis=0
         )
-        terms = dot(factor_grad, entered, 1, 0)
-        for core_half in range(2):
-            for b in range(16):
-                at = core_half * 256 + b * 16
-                to = core_half * 384 + b * 24
-                tail[to : to + 16] += terms[at : at + 16]
-        input_grad = dot(factor_grad, wt_ref[...], 0, 0) + place_of(gate_ref, j)
+        plane_terms[...] = jnp.zeros_like(plane_terms)
+
+        def positions(j):
+            left = plane_flat(turn_a, grads_in[plane, 0, :, :, column(j)].astype(F32))
+            right = plane_flat(turn_b, grads_in[plane, 1, :, :, column(j)].astype(F32))
+            factor_grad = jnp.concatenate(
+                [
+                    left * factor_ref[j, 0, own, :],
+                    left * factor_ref[j, 1, own, :],
+                    right * factor_ref[j, 2, own, :],
+                    right * factor_ref[j, 3, own, :],
+                ],
+                axis=0,
+            ).astype(BF16)
+            plane_terms[...] += dot(factor_grad, entered_ref[j], 1, 0)
+            gate_ref[:, column(j), :] += dot(factor_grad, weights, 0, 0).reshape(8, 128, 128)
+
+        looped(CHUNKS, positions)
+        base = lax.div(zs, 2) * 384 + lax.rem(zs, 2) * 192
+        for b in range(8):
+            tail[pl.ds(pl.multiple_of(base + b * 24, 8), 16)] = plane_terms[b * 16 : b * 16 + 16]
+
+    leave(0, 15)
+    looped(3, lambda i: leave(i + 1, 16))
+
+    def finish(j):
+        normed, inv, _ = enter(j)
+        input_grad = place_of(gate_ref, j)
         tail[16:17] += jnp.sum(input_grad * normed, axis=0, keepdims=True)
         tail[17:18] += jnp.sum(input_grad, axis=0, keepdims=True)
         result = norm_back(input_grad, normed, inv, gain0, 1) + place_of(first_ref, j)
         grad_ref[:, column(j), :] = result.astype(BF16).reshape(8, 128, 128)
 
-    looped(CHUNKS, leave)
+    looped(CHUNKS, finish)
 
     tail_first = send(tail.at[rows(1 - core, 384)], tail_core, send_sems.at[6], recv_sems.at[6], partner)
     tail_first.start()
@@ -438,13 +490,16 @@
     tail_last.start()
 
     def put_proj(which, source):
-        for k in range(2):
-            terms = jnp.concatenate([source[b * 24 : b * 24 + 16] for b in range(8 * k, 8 * k + 8)], axis=0)
-            sum_proj[:, column(which * 2 + k)] = terms.T
+        for k in range(8):
+            at = pl.multiple_of((k % 4) * 128 + (which * 2 + k // 4) * 32, 32)
+            natural[pl.ds(at, 16)] = source[48 * k : 48 * k + 16]
+            natural[pl.ds(at + 16, 16)] = source[48 * k + 24 : 48 * k + 40]
 
     put_proj(core, tail_all)
     tail_last.wait_recv()
     put_proj(1 - core, tail_other)
+    for b in range(4):
+        sum_proj[:, block(b)] = natural[block(b)].T
     norm_terms = jnp.where(core == 0, tail_all[16:24], tail_other[16:24])
     sum_gain[0:1] = norm_terms[0:1]
     sum_bias[0:1] = norm_terms[1:2]
@@ -462,12 +517,13 @@
     tail_last.wait_send()
 
     def settle(j):
-        wait_for(factors_in.at[j, pl.ds(0, 63)], xs.at[0, j])
         wait_for(prod_in.at[j, pl.ds(0, 63)], xs.at[1, j])
         wait_for(cots_in.at[j, pl.ds(0, 63)], xs.at[2, j])
-        wait_for(grads_in.at[j, pl.ds(0, 63)], xs.at[3, j])
 
     looped(CHUNKS, settle)
+    wait_for(factors_in.at[pl.ds(0, 63)], xs.at[0, 0])
+    wait_for(grads_in.at[pl.ds(0, 15)], xs.at[3, 0])
+    looped(3, lambda i: wait_for(grads_in.at[pl.ds(0, 16)], xs.at[3, i + 1]))
 
 
 def local(
@@ -476,7 +532,7 @@
     pair_rows = pair[0]
     cot_rows = cotangent[0]
     vmem = pl.BlockSpec(memory_space=pltpu.VMEM)
-    both = (CHUNKS, 64, 2, 2, 8, 128)
+    both = (64, 2, 2, 8, 512)
     single = (CHUNKS, 64, 2, 8, 128)
     outs = pl.pallas_call(
         functools.partial(whole_kernel, 1.0 / pair_rows.shape[1]),
@@ -532,6 +588,10 @@
             pltpu.VMEM((24, 128), F32),
             pltpu.VMEM((384, 128), F32),
             pltpu.VMEM((384, 128), F32),
+            pltpu.VMEM((CHUNKS, 1024, 128), BF16),
+            pltpu.VMEM((CHUNKS, 4, 128, 1024), F32),
+            pltpu.VMEM((128, 128), F32),
+            pltpu.VMEM((512, 128), F32),
             pltpu.SemaphoreType.DMA((4, CHUNKS)),
             pltpu.SemaphoreType.DMA((4, CHUNKS)),
             pltpu.SemaphoreType.DMA((11,)),

time: 193 us -> 202 us (1.047)
  Pallas kernels: 185 us -> 194 us
    pallas_call x1, Pallas kernels: 185 us -> 194 us  [local(): pl.pallas_call(functools.partial(whole_kernel, 1.0 / pair_rows.shape[1]),...]
where the time goes in v3:
time: 202 us
  Pallas kernels  194 us (96%)
  local copies, waits for them, and re-layouts  6.82 us (3%)
    pallas_call x1, Pallas kernels, local(): pl.pallas_call(functools.partial(whole_kernel, 1.0 / pair_rows.shape[1]),...  194 us
    unnamed x19, local copies, waits for them, and re-layouts  6.82 us

profile of v3, /device:TPU:1, one launch (start us, length us, event | category | flops | bytes accessed | tf_op | source)
XLA Modules:
  0.0 201.9 jit_solution(5510232124482643262)
XLA Ops:
  1.3 193.8 %whole.1 = (bf16[8,512,128]{2,1,0:T(8,128)(2,1)}, f32[128,640]{1,0:T(8,128)}, f32[128,128]{1,0:T(8,128)}, f32[128,512]{1,0:T(8,128)}, f32[512,128]{1,0:T(8,128)}, /*index=5*/f32[3,128]{1,0:T(4,128)}, f32[3,128]{1,0:T(4,128)}) custom-call(s32[1]{0:T(128)S(6)} %copy.23.lengths_ref, bf16[8,512,128]{2,1,0:T(8,128)(2,1)} %bitcast.3, ...), custom_call_target="tpu_custom_call" | custom-call | tf_op jit(solution)/shard_map/whole/pallas_call | solution.py:537
  195.1 0.0 copy-start
  195.1 2.3 %copy.24 = bf16[1,8,512,128]{3,2,1,0:T(8,128)(2,1)} copy(bf16[1,8,512,128]{3,2,1,0:T(8,128)(2,1)} %bitcast.5) | data formatting | bytes 2097152
  197.4 0.0 copy-done
  197.4 0.0 copy-start.3
  197.4 0.0 copy-start.2
  197.4 0.7 copy.25
  198.1 0.1 copy-done.3
  198.3 0.6 copy.26
  198.9 0.0 copy-done.2
  198.9 0.0 copy-start.1
  198.9 0.7 copy.27
  199.6 0.3 copy-done.1
  199.9 0.0 copy-start.5
  199.9 0.7 copy.28
  200.6 0.0 copy-done.5
  200.6 0.0 copy-start.4
  200.6 0.6 copy.29
  201.2 0.1 copy-done.4
  201.3 0.6 copy.30
Async XLA Ops:
  195.1 2.3 %copy-start = (f32[128,640]{1,0:T(8,128)S(1)}, f32[128,640]{1,0:T(8,128)}, u32[]{:S(2)}) copy-start(f32[128,640]{1,0:T(8,128)} %get-tuple-element.29) | copy-start | bytes 983044
  197.4 0.9 copy-start.3
  197.4 1.5 copy-start.2
  198.9 1.0 copy-start.1
  199.9 0.7 copy-start.5
  200.6 0.7 copy-start.4

commit v4 on v2

--- a/solution.py
+++ b/solution.py
@@ -468,6 +468,12 @@
         wait_for(grads_in.at[j, pl.ds(0, 63)], xs.at[3, j])
 
     looped(CHUNKS, settle)
+
+
+def hand_over(*refs):
+    count = len(refs) // 2
+    for source, target in zip(refs[:count], refs[count:]):
+        target[...] = source[...]
 
 
 def local(
@@ -552,6 +558,13 @@
         norm_gain,
         norm_bias,
     )
+    outs = pl.pallas_call(
+        hand_over,
+        out_shape=tuple(jax.ShapeDtypeStruct(o.shape, o.dtype) for o in outs),
+        in_specs=[vmem] * 7,
+        out_specs=(vmem,) * 7,
+        name="hand_over",
+    )(*outs)
     return (outs[0][None], *outs[1:])
 
 

time: 193 us -> 189 us (0.979)
  local copies, waits for them, and re-layouts: 6.82 us -> 0 us
  Pallas kernels: 185 us -> 187 us
    unnamed x19 -> x0, local copies, waits for them, and re-layouts: 6.82 us -> none
    pallas_call x0 -> x1, Pallas kernels: none -> 2.77 us  [local(): pl.pallas_call(hand_over, out_shape=tuple((jax.ShapeDtypeStruct(o.shape,...]
where the time goes in v4:
time: 189 us
  Pallas kernels  187 us (99%)
    pallas_call x1, Pallas kernels, local(): pl.pallas_call(functools.partial(whole_kernel, 1.0 / pair_rows.shape[1]),...  185 us

profile of v4, /device:TPU:1, one launch (start us, length us, event | category | flops | bytes accessed | tf_op | source)
XLA Modules:
  0.0 188.7 jit_solution(5660143504274375099)
XLA Ops:
  1.3 184.6 %whole.1 = (bf16[8,512,128]{2,1,0:T(8,128)(2,1)}, f32[128,640]{1,0:T(8,128)}, f32[128,128]{1,0:T(8,128)}, f32[128,512]{1,0:T(8,128)}, f32[512,128]{1,0:T(8,128)}, /*index=5*/f32[3,128]{1,0:T(4,128)}, f32[3,128]{1,0:T(4,128)}) custom-call(s32[1]{0:T(128)S(6)} %copy.16.lengths_ref, bf16[8,512,128]{2,1,0:T(8,128)(2,1)} %bitcast.3, ...), custom_call_target="tpu_custom_call" | custom-call | tf_op jit(solution)/shard_map/whole/pallas_call | solution.py:487
  185.9 2.8 %hand_over.1 = (bf16[8,512,128]{2,1,0:T(8,128)(2,1)}, f32[128,640]{1,0:T(8,128)}, f32[128,128]{1,0:T(8,128)}, f32[128,512]{1,0:T(8,128)}, f32[512,128]{1,0:T(8,1...) custom-call(bf16[8,512,128]{2,1,0:T(8,128)(2,1)} %get-tuple-element.21.refs_0_, f32[128,640]{1,0:T(8,128)} %get-tuple-element.22.refs_1_, ...), custom_call_target="tpu_custom_call" | custom-call | tf_op jit(solution)/shard_map/hand_over/pallas_call | solution.py:561

commit v5 on v4

--- a/solution.py
+++ b/solution.py
@@ -62,7 +62,11 @@
         dest = lax.rem(q + lax.rem(n, 16), 16) * 4 + lax.rem(z + lax.div(n, 16), 4)
         body(dest, (crop, dest))
 
-    looped(63, step)
+    def steps(i):
+        for k in range(7):
+            step(i * 7 + k)
+
+    looped(9, steps)
 
 
 def sigmoid(x):

time: 189 us -> 190 us (level)
  Pallas kernels: 187 us -> 189 us
where the time goes in v5:
time: 190 us
  Pallas kernels  189 us (99%)
    pallas_call x1, Pallas kernels, local(): pl.pallas_call(functools.partial(whole_kernel, 1.0 / pair_rows.shape[1]),...  186 us

profile of v5, /device:TPU:1, one launch (start us, length us, event | category | flops | bytes accessed | tf_op | source)
XLA Modules:
  0.0 189.8 jit_solution(15868604210984195219)
XLA Ops:
  1.3 185.7 %whole.1 = (bf16[8,512,128]{2,1,0:T(8,128)(2,1)}, f32[128,640]{1,0:T(8,128)}, f32[128,128]{1,0:T(8,128)}, f32[128,512]{1,0:T(8,128)}, f32[512,128]{1,0:T(8,128)}, /*index=5*/f32[3,128]{1,0:T(4,128)}, f32[3,128]{1,0:T(4,128)}) custom-call(s32[1]{0:T(128)S(6)} %copy.16.lengths_ref, bf16[8,512,128]{2,1,0:T(8,128)(2,1)} %bitcast.3, ...), custom_call_target="tpu_custom_call" | custom-call | tf_op jit(solution)/shard_map/whole/pallas_call | solution.py:491
  187.0 2.8 %hand_over.1 = (bf16[8,512,128]{2,1,0:T(8,128)(2,1)}, f32[128,640]{1,0:T(8,128)}, f32[128,128]{1,0:T(8,128)}, f32[128,512]{1,0:T(8,128)}, f32[512,128]{1,0:T(8,1...) custom-call(bf16[8,512,128]{2,1,0:T(8,128)(2,1)} %get-tuple-element.21.refs_0_, f32[128,640]{1,0:T(8,128)} %get-tuple-element.22.refs_1_, ...), custom_call_target="tpu_custom_call" | custom-call | tf_op jit(solution)/shard_map/hand_over/pallas_call | solution.py:565
